TPU v7x, 128 devices: a whole 4x4x4 slice. The times are simulated.
128 devices in a mesh: freq: 8 (over x, z_hi), panel: 16 (over z_lo, y, core).
Axes of the slice: x: 4, y: 4, z: 4 (z_hi: 2, z_lo: 2; z = z_hi * 2 + z_lo), core: 2. Of those that a mesh axis runs over, the one named last changes fastest.
Arguments:
- traces: bfloat16 [640, 640, 1024], P('panel', 'freq'), may hold values from -6 to 6
- filters: float32 [16, 7, 64], replicated, may hold values from -0.25 to 0.25
Outputs:
- primaries: bfloat16 [640, 640, 1024], P('panel', 'freq')
All inputs are finite; a program needn't handle non-finite values.
Results may differ from a plain program's by a relative error of at most 0.0095.
Values may be sent and summed in bfloat16 or wider, within the bound.
No kernel may reach another device: no remote copies, remote signals or barrier semaphores. Data moves between devices by JAX's collectives and lax.ppermute only.
A program may use at most 128 MiB of HBM per device.

v0:
```python
import math
import jax
import jax.numpy as jnp
from jax import lax
from jax.sharding import PartitionSpec as P

NS = 640
NT = 1024
NF = 96
FLO = 8
TAPS = 64
SPAN = 7
RWIN = 40


def wave_table(freq_bins, sample_index):
    phases = freq_bins[:, None] * sample_index[None, :] % NT
    angles = phases.astype(jnp.float32) * jnp.float32(2.0 * math.pi / NT)
    return (jnp.cos(angles), jnp.sin(angles))


def complex_product(left_side, right_side):

    def factor_product(leading_factor, trailing_factor):
        return jnp.einsum(
            "gjo,god->gjd", leading_factor, trailing_factor, preferred_element_type=jnp.float32
        )

    part_real = factor_product(left_side[0], right_side[0]) - factor_product(
        left_side[1], right_side[1]
    )
    part_imag = factor_product(left_side[0], right_side[1]) + factor_product(
        left_side[1], right_side[0]
    )
    return jnp.stack([part_real, part_imag])


def response(filters, freq_bins):
    tap_index = jnp.arange(TAPS, dtype=jnp.int32)
    cosine_wave, sine_wave = wave_table(freq_bins, tap_index)
    filter_real = jnp.einsum("fk,wjk->fjw", cosine_wave, filters)
    filter_imag = -jnp.einsum("fk,wjk->fjw", sine_wave, filters)
    return (jnp.repeat(filter_real, RWIN, axis=2), jnp.repeat(filter_imag, RWIN, axis=2))


def apply_filter(extended, filter_real, filter_imag, source_count):
    sum_real = jnp.zeros(extended.shape[1:2] + (source_count,) + extended.shape[3:], jnp.float32)
    sum_imag = jnp.zeros_like(sum_real)
    for shifted in range(SPAN):
        part_real = extended[0, :, shifted : shifted + source_count, :]
        part_imag = extended[1, :, shifted : shifted + source_count, :]
        weight_real = filter_real[:, shifted][:, None, :]
        weight_imaginary = filter_imag[:, shifted][:, None, :]
        sum_real = sum_real + weight_real * part_real - weight_imaginary * part_imag
        sum_imag = sum_imag + weight_real * part_imag + weight_imaginary * part_real
    return jnp.stack([sum_real, sum_imag])


def per_device(traces, filters):
    shot_rows, receiver_cols, time_sample_count = traces.shape
    rim_width = SPAN // 2
    scale_sources = jnp.float32(math.sqrt(NS))
    freq_bins = FLO + jnp.arange(NF, dtype=jnp.int32)
    cosine_wave, sine_wave = wave_table(freq_bins, jnp.arange(NT, dtype=jnp.int32))
    forward = (jnp.concatenate([cosine_wave, -sine_wave], 0) / jnp.float32(math.sqrt(NT))).astype(
        jnp.bfloat16
    )
    reciprocal_value = jnp.concatenate([cosine_wave, -sine_wave], 0).astype(jnp.bfloat16)
    spectra = jnp.einsum("srt,ct->csr", traces, forward, preferred_element_type=jnp.float32)
    spectra = spectra.astype(jnp.bfloat16).reshape(2, NF, shot_rows, receiver_cols)
    columns = lax.all_to_all(spectra, "panel", split_axis=1, concat_axis=2, tiled=True)
    slice_count = columns.shape[1]
    first_slice = lax.axis_index("panel") * slice_count
    complete = lax.all_gather(columns, "freq", axis=3, tiled=True)
    order_one = (complex_product(complete, columns) / scale_sources).astype(jnp.bfloat16)
    order_two = complex_product(complete, order_one) / scale_sources
    prediction = (order_one.astype(jnp.float32) - order_two).astype(jnp.bfloat16)
    extended = jnp.pad(
        prediction.astype(jnp.float32), ((0, 0), (0, 0), (rim_width, rim_width), (0, 0))
    )
    own_bins = FLO + first_slice + jnp.arange(slice_count, dtype=jnp.int32)
    filter_real, filter_imag = response(filters, own_bins)
    receiver_start = lax.axis_index("freq") * receiver_cols
    filter_real = lax.dynamic_slice_in_dim(filter_real, receiver_start, receiver_cols, 2)
    filter_imag = lax.dynamic_slice_in_dim(filter_imag, receiver_start, receiver_cols, 2)
    matched = apply_filter(extended, filter_real, filter_imag, NS)
    returned = lax.all_to_all(
        matched.astype(jnp.bfloat16), "panel", split_axis=2, concat_axis=1, tiled=True
    )
    matched_rows = returned.reshape(2 * NF, shot_rows, receiver_cols)
    multiples = jnp.einsum(
        "csr,ct->srt", matched_rows, reciprocal_value, preferred_element_type=jnp.float32
    )
    multiples = multiples / jnp.float32(math.sqrt(NF))
    return (traces.astype(jnp.float32) - multiples).astype(jnp.bfloat16)


def solution(mesh):
    placed = (P("panel", "freq", None), P())
    return jax.shard_map(
        per_device, mesh=mesh, in_specs=placed, out_specs=P("panel", "freq", None), check_vma=False
    )
```

profile of v0, /device:TPU:1, one launch (start us, length us, event | category | flops | bytes accessed | tf_op | source)
XLA Modules:
  0.0 312.2 jit_solution(14349941599640643925)
XLA Ops:
  6.5 1.6 fusion.58
  8.2 0.8 copy-done.4
  9.1 4.8 %convolution_convert_fusion = bf16[192,40,80]{0,2,1:T(8,128)(2,1)S(1)} fusion(bf16[40,80,1024]{2,1,0:T(8,128)(2,1)} %param.2, f32[96,1024]{1,0:T(8,128)S(1)} %get-tuple-element.24, f32[96,1024]{1,0:T(8,128)S(1)} %get-tuple-element.23), kind=kOutput, calls=%fused_computation.35 | convolution fusion | flops 1259495424 | bytes 8568832 | tf_op jit(solution)/shard_map/srt,ct->csr/dot_general | solution.py:69
  13.9 0.9 reshape.26
  14.7 3.3 %copy.54 = bf16[2,96,40,80]{3,2,0,1:T(8,128)(2,1)} copy(bf16[2,96,40,80]{1,0,3,2:T(2,128)(2,1)S(1)} %reshape.26) | data formatting | bytes 2457600 | tf_op jit(solution)/shard_map/reshape | solution.py:70
  18.1 32.3 %all_to_all.33 = bf16[2,96,40,80]{3,2,0,1:T(8,128)(2,1)S(1)} all-to-all(bf16[2,96,40,80]{3,2,0,1:T(8,128)(2,1)} %copy.54), channel_id=1, replica_groups=mesh['freq'=8,'panel'=16] {'panel'}, dimensions={1} | all-to-all | bytes 2457600 | tf_op jit(solution)/shard_map/all_to_all | solution.py:71
  50.4 1.7 copy.56
  52.2 4.5 %copy.57 = bf16[2,6,640,80]{2,0,1,3:T(2,128)(2,1)} copy(bf16[2,6,640,80]{3,2,1,0:T(8,128)(2,1)} %bitcast.140) | data formatting | bytes 2457600 | tf_op jit(solution)/shard_map/all_to_all | solution.py:71
  58.4 0.3 copy.55
  58.7 0.3 fusion.81
  59.3 118.6 %all-gather.2.cloned.1.call-done = bf16[2,6,640,640]{2,0,1,3:T(2,128)(2,1)} async-done(((bf16[2,6,640,80]{2,0,1,3:T(2,128)(2,1)}), bf16[2,6,640,640]{2,0,1,3:T(2,128)(2,1)}) %all-gather.2.cloned.1.call-update) | async-done | bytes 9830416 | tf_op jit(solution)/shard_map/all_gather | solution.py:74
  177.9 20.6 %fusion.80 = (bf16[1,6,640,640]{2,0,1,3:T(2,128)(2,1)}, bf16[1,6,640,640]{2,0,1,3:T(2,128)(2,1)}) fusion(bf16[2,6,640,640]{2,0,1,3:T(2,128)(2,1)} %all-gather.2.cloned.1.call-done), kind=kLoop, calls=%fused_computation.122 | loop fusion | bytes 19660800 | tf_op jit(solution)/shard_map/slice | solution.py:29
  198.5 19.7 %copy.91 = bf16[1,6,640,640]{3,2,1,0:T(8,128)(2,1)} copy(bf16[1,6,640,640]{2,0,1,3:T(2,128)(2,1)} %get-tuple-element.6) | data formatting | bytes 9830400
  218.3 19.8 %copy.90 = bf16[1,6,640,640]{3,2,1,0:T(8,128)(2,1)} copy(bf16[1,6,640,640]{2,0,1,3:T(2,128)(2,1)} %get-tuple-element.5) | data formatting | bytes 9830400
  238.0 4.2 %fusion.6 = f32[6,640,80]{1,2,0:T(8,128)S(1)} fusion(bf16[6,640,80]{2,1,0:T(8,128)(2,1)S(1)} %bitcast.133, bf16[1,6,640,640]{3,2,1,0:T(8,128)(2,1)} %copy.91), kind=kOutput, calls=%fused_computation.7 | convolution fusion | flops 393216000 | bytes 6758400 | tf_op jit(solution)/shard_map/gjo,god->gjd/dot_general | solution.py:25
  242.2 1.7 fusion.4
  243.9 0.7 copy-done.3
  244.6 1.7 fusion.23
  246.3 1.7 fusion.29
  248.2 1.7 fusion.2
  249.8 1.7 fusion
  251.5 1.7 fusion.35
  253.2 1.7 fusion.41
  254.8 0.4 fusion.44
  255.2 5.4 %subtract_convert_fusion.1 = bf16[1,6,640,80]{2,3,1,0:T(8,128)(2,1)S(1)} fusion(f32[2,6,640,80]{2,3,1,0:T(8,128)S(1)} %fusion.44, f32[6,80]{1,0:T(8,128)S(1)} %bitcast.143, f32[6,80]{1,0:T(8,128)S(1)} %bitcast.145, f32[6,80]{1,0:T(8,128)S(1)} %bitcast.147, f32[6,80]{1,0:T(8,128)S(1)} %bitcast.149, f32[6,80]{1,0:T(8,128)S(1)} %bitcast.151, ...), kind=kLoop, calls=%fused_computation.47 | loop fusion | flops 8601600 | bytes 5586944 | tf_op jit(solution)/shard_map/convert
  260.6 5.3 %add_convert_fusion = bf16[1,6,640,80]{2,3,1,0:T(8,128)(2,1)S(1)} fusion(f32[2,6,640,80]{2,3,1,0:T(8,128)S(1)} %fusion.44, f32[6,80]{1,0:T(8,128)S(1)} %bitcast.144, f32[6,80]{1,0:T(8,128)S(1)} %bitcast.146, f32[6,80]{1,0:T(8,128)S(1)} %bitcast.148, f32[6,80]{1,0:T(8,128)S(1)} %bitcast.150, f32[6,80]{1,0:T(8,128)S(1)} %bitcast.152, ...), kind=kLoop, calls=%fused_computation.46 | loop fusion | flops 8601600 | bytes 5586944 | tf_op jit(solution)/shard_map/convert.1
  266.1 2.6 copy.67
  268.7 30.9 %all_to_all.34 = bf16[2,6,640,80]{3,0,1,2:T(2,128)(2,1)S(1)} all-to-all(bf16[2,6,640,80]{3,0,1,2:T(2,128)(2,1)S(1)} %copy.67), channel_id=1, replica_groups=mesh['freq'=8,'panel'=16] {'panel'}, dimensions={2} | all-to-all | bytes 2457600 | tf_op jit(solution)/shard_map/all_to_all | solution.py:87
  299.5 0.4 copy.68
  299.9 0.3 copy.69
  300.3 0.9 slice-done.1
  301.4 4.0 %subtract_convert_fusion = bf16[40,80,1024]{2,1,0:T(8,128)(2,1)} fusion(bf16[40,80,1024]{2,1,0:T(8,128)(2,1)S(1)} %bitcast.142, bf16[192,40,80]{2,1,0:T(8,128)(2,1)S(1)} %bitcast.138, f32[96,1024]{1,0:T(8,128)S(1)} %copy-done.7, f32[96,1024]{1,0:T(8,128)S(1)} %copy-done.5), kind=kOutput, calls=%fused_computation | convolution fusion | flops 1272184832 | bytes 15122432 | tf_op jit(solution)/shard_map/csr,ct->srt/dot_general | solution.py:91
  (49 shorter events, 2.5 us)
Async XLA Ops:
  6.5 50.2 %copy-start = (f32[16,7,64]{2,0,1:T(8,128)S(1)}, f32[16,7,64]{2,0,1:T(8,128)}, u32[]{:S(2)}) copy-start(f32[16,7,64]{2,0,1:T(8,128)} %param.3) | copy-start | bytes 86020
  6.5 171.3 %all-gather.2.cloned.1.call-start = ((), (), s32[]{:S(2)}) async-start(), calls=%async_computation.2 | async-start | bytes 11059200 | tf_op jit(solution)/shard_map/all_gather | solution.py:74
  8.2 0.8 copy-start.4
  8.2 0.9 copy-start.6
  238.0 4.2 %copy-start.2 = (bf16[1,6,640,640]{3,2,1,0:T(8,128)(2,1)S(1)}, bf16[1,6,640,640]{3,2,1,0:T(8,128)(2,1)}, u32[]{:S(2)}) copy-start(bf16[1,6,640,640]{3,2,1,0:T(8,128)(2,1)} %copy.91) | copy-start | bytes 14745604
  242.2 2.4 copy-start.3
  268.6 31.6 %slice-start = ((s8[6553600]{0:T(1024)(128)(4,1)}), s8[4194304]{0:T(1024)(128)(4,1)S(1)}, s32[]{:S(2)}) async-start(s8[6553600]{0:T(1024)(128)(4,1)} %bitcast.141), calls=%async_computation.3 | async-start | bytes 8388608
  299.5 1.7 slice-start.1
  299.9 1.4 copy-start.5
  299.9 1.5 copy-start.7
  301.4 4.0 %copy-start.1 = (f32[16,7,64]{2,0,1:T(8,128)S(1)}, f32[16,7,64]{2,0,1:T(8,128)}, u32[]{:S(2)}) copy-start(f32[16,7,64]{2,0,1:T(8,128)} %param.3) | copy-start | bytes 86020
Sparse Core Ops, SparseCore 0:
  56.8 120.9 all-gather.1
where the time goes:
time: 314 us; the launch traced here: 312 us
  waiting for transfers between devices  119 us (38%)
  local copies, waits for them, and re-layouts  78.6 us (25%)
  blocking collectives  63.2 us (20%)
  matrix products  25 us (8%)
  between operations  13.7 us (4%)
  other arithmetic  13.1 us (4%)
    all_gather x1, waiting for transfers between devices, per_device(): complete = lax.all_gather(columns, 'freq', axis=3, tiled=True)  119 us
    unnamed x36, local copies, waits for them, and re-layouts  42.4 us
    all_to_all x1, blocking collectives, per_device(): lax.all_to_all(spectra, 'panel', split_axis=1, concat_axis=2, tiled=True)  32.3 us
    all_to_all x1, blocking collectives, per_device(): lax.all_to_all(matched.astype(jnp.bfloat16), 'panel', split_axis=2, conca...  30.9 us
    slice x1, local copies, waits for them, and re-layouts, complex_product(): left_side[0]  20.6 us
    dot_general x8, matrix products, factor_product(): jnp.einsum('gjo,god->gjd', leading_factor, trailing_factor, preferred_ele...  15.8 us
    another operation x2, other arithmetic  10.7 us
    all_to_all x3, local copies, waits for them, and re-layouts, per_device(): lax.all_to_all(spectra, 'panel', split_axis=1, concat_axis=2, tiled=True)  6.6 us
  transfers between devices with their start and end apart: 1, of which 1 were waited for; matrix products, arithmetic and copies ran while one was open for 1% of the time, Pallas kernels for 0%

commit v1 on v0

--- a/solution.py
+++ b/solution.py
@@ -11,6 +11,15 @@
 TAPS = 64
 SPAN = 7
 RWIN = 40
+
+
+def spread_point(row_data, named_axis, d0):
+    gallery = []
+    for _ in range(lax.axis_size(named_axis)):
+        gallery.append(row_data)
+    mixed_arr = jnp.stack(gallery, 0)
+    right_arr = lax.all_to_all(mixed_arr, axis_name=named_axis, split_axis=0, concat_axis=0)
+    return jnp.concatenate(right_arr, axis=d0)
 
 
 def wave_table(freq_bins, sample_index):
@@ -71,7 +80,7 @@
     columns = lax.all_to_all(spectra, "panel", split_axis=1, concat_axis=2, tiled=True)
     slice_count = columns.shape[1]
     first_slice = lax.axis_index("panel") * slice_count
-    complete = lax.all_gather(columns, "freq", axis=3, tiled=True)
+    complete = spread_point(columns, "freq", d0=3)
     order_one = (complex_product(complete, columns) / scale_sources).astype(jnp.bfloat16)
     order_two = complex_product(complete, order_one) / scale_sources
     prediction = (order_one.astype(jnp.float32) - order_two).astype(jnp.bfloat16)

time: 314 us -> 271 us (0.86)
  local copies, waits for them, and re-layouts: 78.6 us -> 36.4 us
  between operations: 13.7 us -> 0.39 us
  waiting for transfers between devices: 119 us -> 132 us
  starting transfers between devices: 0.01 us -> 7.04 us
  matrix products: 25 us -> 19.6 us
    all_to_all x0 -> x1, waiting for transfers between devices: none -> 132 us  [spread_point(): lax.all_to_all(mixed_arr, axis_name=named_axis, split_axis=0, concat_axis=0)]
    all_gather x1 -> x0, waiting for transfers between devices: 119 us -> none  [per_device(): complete = lax.all_gather(columns, 'freq', axis=3, tiled=True)]
    unnamed x36 -> x32, local copies, waits for them, and re-layouts: 42.4 us -> 2.41 us
    slice x1, local copies, waits for them, and re-layouts: 20.6 us -> 6.98 us  [complex_product(): left_side[1]]
    all_to_all x0 -> x1, local copies, waits for them, and re-layouts: none -> 8.72 us  [spread_point(): lax.all_to_all(mixed_arr, axis_name=named_axis, split_axis=0, concat_axis=0)]
    another operation x0 -> x2, local copies, waits for them, and re-layouts: none -> 7.27 us  [spread_point(): mixed_arr = jnp.stack(gallery, 0)]
    all_to_all x0 -> x1, starting transfers between devices: none -> 7.04 us  [spread_point(): lax.all_to_all(mixed_arr, axis_name=named_axis, split_axis=0, concat_axis=0)]
    dot_general x8, matrix products: 15.8 us -> 10.4 us  [factor_product(): jnp.einsum('gjo,god->gjd', leading_factor, trailing_factor, preferred_ele...]
where the time goes in v1:
time: 271 us
  waiting for transfers between devices  132 us (49%)
  blocking collectives  62.4 us (23%)
  local copies, waits for them, and re-layouts  36.4 us (13%)
  matrix products  19.6 us (7%)
  other arithmetic  13.3 us (5%)
  starting transfers between devices  7.04 us (3%)
    all_to_all x1, waiting for transfers between devices, spread_point(): lax.all_to_all(mixed_arr, axis_name=named_axis, split_axis=0, concat_axis=0)  132 us
    all_to_all x1, blocking collectives, per_device(): lax.all_to_all(spectra, 'panel', split_axis=1, concat_axis=2, tiled=True)  32.4 us
    all_to_all x1, blocking collectives, per_device(): lax.all_to_all(matched.astype(jnp.bfloat16), 'panel', split_axis=2, conca...  30 us
    another operation x2, other arithmetic  10.9 us
    dot_general x8, matrix products, factor_product(): jnp.einsum('gjo,god->gjd', leading_factor, trailing_factor, preferred_ele...  10.4 us
    all_to_all x1, local copies, waits for them, and re-layouts, spread_point(): lax.all_to_all(mixed_arr, axis_name=named_axis, split_axis=0, concat_axis=0)  8.72 us
    another operation x2, local copies, waits for them, and re-layouts, spread_point(): mixed_arr = jnp.stack(gallery, 0)  7.27 us
    all_to_all x1, starting transfers between devices, spread_point(): lax.all_to_all(mixed_arr, axis_name=named_axis, split_axis=0, concat_axis=0)  7.04 us
  transfers between devices with their start and end apart: 1, of which 1 were waited for; matrix products, arithmetic and copies ran while one was open for 1% of the time, Pallas kernels for 0%

profile of v1, /device:TPU:1, one launch (start us, length us, event | category | flops | bytes accessed | tf_op | source)
XLA Modules:
  0.0 270.8 jit_solution(7768147361453043003)
XLA Ops:
  0.0 1.6 fusion.24
  1.6 0.7 copy-done.3
  2.5 4.8 %convolution_convert_fusion = bf16[192,40,80]{0,2,1:T(8,128)(2,1)S(1)} fusion(bf16[40,80,1024]{2,1,0:T(8,128)(2,1)} %param.2, f32[96,1024]{1,0:T(8,128)S(1)} %get-tuple-element.24, f32[96,1024]{1,0:T(8,128)S(1)} %get-tuple-element.23), kind=kOutput, calls=%fused_computation.20 | convolution fusion | flops 1259495424 | bytes 8568832 | tf_op jit(solution)/shard_map/srt,ct->csr/dot_general | solution.py:78
  7.3 0.9 reshape.37
  8.1 3.3 %copy.54 = bf16[2,96,40,80]{3,2,0,1:T(8,128)(2,1)} copy(bf16[2,96,40,80]{1,0,3,2:T(2,128)(2,1)S(1)} %reshape.37) | data formatting | bytes 2457600 | tf_op jit(solution)/shard_map/reshape | solution.py:79
  11.5 32.4 %all_to_all.35 = bf16[2,96,40,80]{3,2,0,1:T(8,128)(2,1)S(1)} all-to-all(bf16[2,96,40,80]{3,2,0,1:T(8,128)(2,1)} %copy.54), channel_id=1, replica_groups=mesh['freq'=8,'panel'=16] {'panel'}, dimensions={1} | all-to-all | bytes 2457600 | tf_op jit(solution)/shard_map/all_to_all | solution.py:80
  43.8 1.7 copy.56
  45.6 2.7 %copy.57 = bf16[2,6,640,80]{2,3,1,0:T(8,128)(2,1)S(1)} copy(bf16[2,6,640,80]{3,2,1,0:T(8,128)(2,1)} %bitcast.128) | data formatting | bytes 2457600 | tf_op jit(solution)/shard_map/stack | solution.py:20
  48.3 4.6 %stack.38 = bf16[8,2,6,640,80]{3,4,2,1,0:T(8,128)(2,1)} broadcast(bf16[2,6,640,80]{2,3,1,0:T(8,128)(2,1)S(1)} %copy.57), dimensions={1,2,3,4} | broadcast | bytes 11059200 | tf_op jit(solution)/shard_map/stack | solution.py:20
  52.8 7.0 %all-to-all-start.1 = ((bf16[8,2,6,640,80]{3,4,2,1,0:T(8,128)(2,1)}), bf16[8,2,6,640,80]{3,4,2,1,0:T(8,128)(2,1)}, u32[]{:S(2)}, u32[]{:S(2)}) async-start(bf16[8,2,6,640,80]{3,4,2,1,0:T(8,128)(2,1)} %stack.38), calls=%async_computation.1 | async-start | bytes 19660800 | tf_op jit(solution)/shard_map/all_to_all | solution.py:21
  61.5 0.3 copy.55
  61.9 0.3 fusion.47
  62.4 131.7 %all-to-all-done.1 = bf16[8,2,6,640,80]{3,4,2,1,0:T(8,128)(2,1)} async-done(((bf16[8,2,6,640,80]{3,4,2,1,0:T(8,128)(2,1)}), bf16[8,2,6,640,80]{3,4,2,1,0:T(8,128)(2,1)}, u32[]{:S(2)}, u32[]{:S(2)}) %all-to-all-start.1) | async-done | bytes 9830432 | tf_op jit(solution)/shard_map/all_to_all | solution.py:21
  194.2 8.7 %copy.122 = bf16[8,2,6,640,80]{3,4,0,2,1:T(8,128)(2,1)} copy(bf16[8,2,6,640,80]{3,4,2,1,0:T(8,128)(2,1)} %all-to-all-done.1) | data formatting | bytes 19660800 | tf_op jit(solution)/shard_map/all_to_all | solution.py:21
  202.9 7.0 %fusion.46 = (bf16[1,6,640,8,80]{2,4,3,1,0:T(8,128)(2,1)S(1)}, bf16[1,6,640,8,80]{2,4,3,1,0:T(8,128)(2,1)}) fusion(bf16[2,6,640,8,80]{2,4,3,1,0:T(8,128)(2,1)} %bitcast.119), kind=kLoop, calls=%fused_computation.109 | loop fusion | bytes 19660800 | tf_op jit(solution)/shard_map/slice | solution.py:39
  209.9 3.5 %fusion.50 = f32[6,640,80]{1,2,0:T(8,128)S(1)} fusion(bf16[6,640,640]{1,2,0:T(8,128)(2,1)} %bitcast.115, bf16[6,640,80]{2,1,0:T(8,128)(2,1)S(1)} %bitcast.121), kind=kOutput, calls=%fused_computation.113 | convolution fusion | flops 393216000 | bytes 6758400 | tf_op jit(solution)/shard_map/gjo,god->gjd/dot_general | solution.py:34
  213.7 1.0 fusion.51
  214.7 1.0 fusion.4
  215.7 1.0 fusion.5
  217.0 1.0 fusion.11
  217.9 1.0 fusion.12
  218.9 1.0 fusion.6
  219.9 1.0 fusion.7
  220.9 0.4 fusion.8
  221.2 5.6 %subtract_convert_fusion.1 = bf16[1,6,640,80]{2,3,1,0:T(8,128)(2,1)S(1)} fusion(f32[2,6,640,80]{2,3,1,0:T(8,128)S(1)} %fusion.8, f32[6,80]{1,0:T(8,128)S(1)} %bitcast.153, f32[6,80]{1,0:T(8,128)S(1)} %bitcast.155, f32[6,80]{1,0:T(8,128)S(1)} %bitcast.157, f32[6,80]{1,0:T(8,128)S(1)} %bitcast.131, f32[6,80]{1,0:T(8,128)S(1)} %bitcast.133, ...), kind=kLoop, calls=%fused_computation.32 | loop fusion | flops 8601600 | bytes 5586944 | tf_op jit(solution)/shard_map/convert
  226.8 5.3 %add_convert_fusion = bf16[1,6,640,80]{2,3,1,0:T(8,128)(2,1)S(1)} fusion(f32[2,6,640,80]{2,3,1,0:T(8,128)S(1)} %fusion.8, f32[6,80]{1,0:T(8,128)S(1)} %bitcast.154, f32[6,80]{1,0:T(8,128)S(1)} %bitcast.156, f32[6,80]{1,0:T(8,128)S(1)} %bitcast.158, f32[6,80]{1,0:T(8,128)S(1)} %bitcast.132, f32[6,80]{1,0:T(8,128)S(1)} %bitcast.134, f32[6,80]{1,0:T(8,128)S(1)} %bitcast.136, ...), kind=kLoop, calls=%fused_computation.31 | loop fusion | flops 8601600 | bytes 5586944 | tf_op jit(solution)/shard_map/convert.1
  232.3 2.6 copy.74
  234.9 30.0 %all_to_all.36 = bf16[2,6,640,80]{3,0,1,2:T(2,128)(2,1)S(1)} all-to-all(bf16[2,6,640,80]{3,0,1,2:T(2,128)(2,1)S(1)} %copy.74), channel_id=1, replica_groups=mesh['freq'=8,'panel'=16] {'panel'}, dimensions={2} | all-to-all | bytes 2457600 | tf_op jit(solution)/shard_map/all_to_all | solution.py:96
  264.9 0.4 copy.75
  265.3 0.3 copy.76
  265.6 0.9 slice-done.1
  266.8 4.0 %subtract_convert_fusion = bf16[40,80,1024]{2,1,0:T(8,128)(2,1)} fusion(bf16[40,80,1024]{2,1,0:T(8,128)(2,1)S(1)} %bitcast.130, bf16[192,40,80]{2,1,0:T(8,128)(2,1)S(1)} %bitcast.126, f32[96,1024]{1,0:T(8,128)S(1)} %copy-done.6, f32[96,1024]{1,0:T(8,128)S(1)} %copy-done.4), kind=kOutput, calls=%fused_computation | convolution fusion | flops 1272184832 | bytes 15122432 | tf_op jit(solution)/shard_map/csr,ct->srt/dot_general | solution.py:100
  (46 shorter events, 2.8 us)
Async XLA Ops:
  0.0 59.9 %copy-start = (f32[16,7,64]{2,0,1:T(8,128)S(1)}, f32[16,7,64]{2,0,1:T(8,128)}, u32[]{:S(2)}) copy-start(f32[16,7,64]{2,0,1:T(8,128)} %param.3) | copy-start | bytes 86020
  1.6 0.7 copy-start.3
  1.6 0.9 copy-start.5
  52.8 141.3 %all-to-all-start.1 = ((bf16[8,2,6,640,80]{3,4,2,1,0:T(8,128)(2,1)}), bf16[8,2,6,640,80]{3,4,2,1,0:T(8,128)(2,1)}, u32[]{:S(2)}, u32[]{:S(2)}) async-start(bf16[8,2,6,640,80]{3,4,2,1,0:T(8,128)(2,1)} %stack.38), calls=%async_computation.1 | async-start | bytes 19660800 | tf_op jit(solution)/shard_map/all_to_all | solution.py:21
  209.9 3.9 %copy-start.2 = (bf16[1,6,640,8,80]{2,4,3,1,0:T(8,128)(2,1)S(1)}, bf16[1,6,640,8,80]{2,4,3,1,0:T(8,128)(2,1)}, u32[]{:S(2)}) copy-start(bf16[1,6,640,8,80]{2,4,3,1,0:T(8,128)(2,1)} %get-tuple-element.6) | copy-start | bytes 14745604
  234.9 30.7 %slice-start = ((s8[6553600]{0:T(1024)(128)(4,1)}), s8[4194304]{0:T(1024)(128)(4,1)S(1)}, s32[]{:S(2)}) async-start(s8[6553600]{0:T(1024)(128)(4,1)} %bitcast.129), calls=%async_computation.3 | async-start | bytes 8388608
  264.9 1.7 slice-start.1
  265.3 1.4 copy-start.4
  265.3 1.5 copy-start.6
  266.8 4.0 %copy-start.1 = (f32[16,7,64]{2,0,1:T(8,128)S(1)}, f32[16,7,64]{2,0,1:T(8,128)}, u32[]{:S(2)}) copy-start(f32[16,7,64]{2,0,1:T(8,128)} %param.3) | copy-start | bytes 86020
